TPU v7x, 32 devices: a whole 2x2x4 slice. The times are simulated.
32 devices in a mesh: section: 2 (over x), seq: 8 (over z, y), rep: 2 (over core).
Axes of the slice: x: 2, y: 2, z: 4, core: 2. Of those that a mesh axis runs over, the one named last changes fastest.
Arguments:
- queries: bfloat16 [512, 2560], P('seq', ('section', 'rep')), may hold values from -5 to 5
- keys: bfloat16 [512, 2560], P('seq', ('section', 'rep')), may hold values from -5 to 5
- values: bfloat16 [512, 2560], P('seq', ('section', 'rep')), may hold values from -6 to 6
- block_order: int32 [16], replicated, may hold values from 0 to 15, each once
- wo: bfloat16 [2560, 5120], P(('section', 'rep'), 'seq'), may hold values from -0.125 to 0.125
- resid: bfloat16 [4, 5120, 128], P(('section', 'rep'), 'seq'), may hold values from -60 to 60
- gain: bfloat16 [5120], P('seq'), may hold values from 0.099609375 to 1.8984375
- w_gate: bfloat16 [13824, 5120], P('seq'), may hold values from -0.078125 to 0.078125
- w_up: bfloat16 [13824, 5120], P('seq'), may hold values from -0.078125 to 0.078125
- w_down: bfloat16 [13824, 5120], P('seq'), may hold values from -0.0625 to 0.0625
Outputs:
- mixed: bfloat16 [4, 5120, 128], P(('section', 'rep'), 'seq')
Inputs may be any that keep to these rules, and one draw needn't show every extreme that they name: `block_order`: each number once.
All inputs are finite; a program needn't handle non-finite values.
Results may differ from a plain program's by a relative error of at most 0.0055.
Values may be sent and summed in bfloat16 or wider, within the bound.
A program may use at most 128 MiB of HBM per device.

v0:
```python
import jax
import jax.numpy as jnp
from jax import lax
from jax.sharding import PartitionSpec as P

D = 5120
HEAD_DIM = 128


def key_positions(order, start, count, block_rows):
    row_ids = start + jnp.arange(count, dtype=jnp.int32)
    owners = row_ids // block_rows
    match = owners[:, None] == jnp.arange(order.shape[0], dtype=jnp.int32)[None, :]
    first = jnp.sum(jnp.where(match, order[None, :], 0), axis=1)
    return first * block_rows + row_ids % block_rows


def on_device(queries, keys, values, block_order, wo, resid, gain, w_gate, w_up, w_down):
    seq_dev = queries.shape[0]
    heads_dev = queries.shape[1] // HEAD_DIM
    groups = lax.axis_size("section") * lax.axis_size("rep")
    n_seq = lax.axis_size("seq")
    sub_rows = seq_dev // groups
    block_rows = seq_dev // 2
    query_start = lax.axis_index("seq") * seq_dev
    query_pos = key_positions(block_order, query_start, seq_dev, block_rows)
    query_heads = queries.reshape(seq_dev, heads_dev, HEAD_DIM)
    scale = HEAD_DIM ** (-0.5)
    running_max = jnp.full((seq_dev, heads_dev), -1e30, jnp.float32)
    key_piece = lax.all_gather(keys, "seq", axis=0, tiled=True)
    value_piece = lax.all_gather(values, "seq", axis=0, tiled=True)
    count = key_piece.shape[0]
    key_pos = key_positions(block_order, jnp.int32(0), count, block_rows)
    scores = (
        jnp.einsum(
            "qhd,khd->qhk",
            query_heads,
            key_piece.reshape(count, heads_dev, HEAD_DIM),
            preferred_element_type=jnp.float32,
        )
        * scale
    )
    visible = (key_pos[None, :] <= query_pos[:, None])[:, None, :]
    new_max = jnp.maximum(running_max, jnp.max(jnp.where(visible, scores, -1e30), axis=-1))
    probs = jnp.where(visible, jnp.exp(scores - new_max[..., None]), 0.0)
    total = jnp.sum(probs, axis=-1)
    weighted = jnp.einsum(
        "qhk,khd->qhd",
        probs.astype(jnp.bfloat16),
        value_piece.reshape(count, heads_dev, HEAD_DIM),
        preferred_element_type=jnp.float32,
    )
    running_max, total, weighted = (new_max, total, weighted)
    attended = (
        (weighted / total[..., None]).astype(jnp.bfloat16).reshape(seq_dev, heads_dev * HEAD_DIM)
    )
    columns = wo.shape[1]
    token_count = n_seq * sub_rows
    parts = attended.reshape(groups, sub_rows, heads_dev * HEAD_DIM)
    group_rows = lax.all_to_all(parts, ("section", "rep"), split_axis=0, concat_axis=2, tiled=True)
    wo_columns = lax.all_gather(wo, ("section", "rep"), axis=0, tiled=True)
    piece = lax.all_gather(group_rows, "seq", axis=0, tiled=True)
    flat = piece.reshape(piece.shape[0] * piece.shape[1], piece.shape[2])
    product = jnp.dot(flat, wo_columns, preferred_element_type=jnp.float32)
    projected = product.reshape(piece.shape[0], piece.shape[1], columns)
    projected_cols = projected.reshape(token_count, columns).T
    carried = resid.reshape(columns, token_count).astype(jnp.float32) + projected_cols
    squares = lax.psum(jnp.sum(carried * carried, axis=0), "seq")
    normed = (
        carried * lax.rsqrt(squares / D + 1e-05)[None, :] * gain.astype(jnp.float32)[:, None]
    ).astype(jnp.bfloat16)
    piece = lax.all_gather(normed, "seq", axis=0, tiled=True)
    gate_sum = jnp.dot(w_gate, piece, preferred_element_type=jnp.float32)
    up_sum = jnp.dot(w_up, piece, preferred_element_type=jnp.float32)
    hidden = (jax.nn.silu(gate_sum) * up_sum).astype(jnp.bfloat16)
    term = lax.dot_general(
        w_down, hidden, (((0,), (0,)), ((), ())), preferred_element_type=jnp.float32
    )
    down = lax.psum_scatter(term, "seq", scatter_dimension=0, tiled=True)
    return (carried + down).astype(jnp.bfloat16).reshape(resid.shape)


def solution(mesh):
    return jax.shard_map(
        on_device,
        mesh=mesh,
        in_specs=(
            P("seq", ("section", "rep")),
            P("seq", ("section", "rep")),
            P("seq", ("section", "rep")),
            P(),
            P(("section", "rep"), "seq"),
            P(("section", "rep"), "seq", None),
            P("seq"),
            P("seq", None),
            P("seq", None),
            P("seq", None),
        ),
        out_specs=P(("section", "rep"), "seq", None),
        check_vma=False,
    )
```

profile of v0, /device:TPU:0, one launch (start us, length us, event | category | flops | bytes accessed | tf_op | source)
XLA Modules:
  0.0 288.4 jit_solution(9217807981591576571)
XLA Ops:
  6.5 0.7 all-gather.3.cloned.1.call-update
  7.3 33.6 %all_gather.15 = bf16[512,640]{1,0:T(8,128)(2,1)S(1)} all-gather(bf16[64,640]{1,0:T(8,128)(2,1)} %param.11), channel_id=1, replica_groups=mesh['section'=2,'seq'=8,'rep'=2] {'seq'}, dimensions={0}, use_global_device_ids=true | all-gather | bytes 737280 | tf_op jit(solution)/shard_map/all_gather | solution.py:30
  40.9 0.3 copy.33
  41.2 31.9 %all_gather.16 = bf16[512,640]{1,0:T(8,128)(2,1)S(1)} all-gather(bf16[64,640]{1,0:T(8,128)(2,1)} %param.12), channel_id=1, replica_groups=mesh['section'=2,'seq'=8,'rep'=2] {'seq'}, dimensions={0}, use_global_device_ids=true | all-gather | bytes 737280 | tf_op jit(solution)/shard_map/all_gather | solution.py:31
  73.1 0.3 copy.36
  73.4 0.1 select_reduce_fusion.2
  73.5 0.1 select_reduce_fusion.1
  73.7 0.3 select_reduce_fusion
  74.0 0.3 fusion.6
  74.3 0.4 fusion.5
  74.7 0.7 reshape_reshape.3
  75.5 3.3 %all-to-all-start = ((bf16[4,16,640]{2,1,0:T(8,128)(2,1)}), bf16[4,16,640]{2,1,0:T(8,128)(2,1)S(1)}, u32[]{:S(2)}, u32[]{:S(2)}) async-start(bf16[4,16,640]{2,1,0:T(8,128)(2,1)} %reshape_reshape.3), calls=%async_computation | async-start | bytes 163840 | tf_op jit(solution)/shard_map/all_to_all | solution.py:60
  78.9 0.2 copy.32
  79.0 3.9 %all-to-all-done = bf16[4,16,640]{2,1,0:T(8,128)(2,1)S(1)} async-done(((bf16[4,16,640]{2,1,0:T(8,128)(2,1)}), bf16[4,16,640]{2,1,0:T(8,128)(2,1)S(1)}, u32[]{:S(2)}, u32[]{:S(2)}) %all-to-all-start) | async-done | bytes 81952 | tf_op jit(solution)/shard_map/all_to_all | solution.py:60
  83.0 31.7 %all_gather.17 = bf16[8,16,2560]{2,1,0:T(8,128)(2,1)S(1)} all-gather(bf16[1,16,2560]{2,1,0:T(8,128)(2,1)S(1)} %bitcast.59), channel_id=1, replica_groups=mesh['section'=2,'seq'=8,'rep'=2] {'seq'}, dimensions={0}, use_global_device_ids=true | all-gather | bytes 737280 | tf_op jit(solution)/shard_map/all_gather | solution.py:62
  114.6 2.7 multiply_reduce_fusion
  117.3 21.5 %psum.7 = f32[128]{0:T(128)S(1)} all-reduce(f32[128]{0:T(128)S(1)} %get-tuple-element.7), channel_id=1, replica_groups=mesh['section'=2,'seq'=8,'rep'=2] {'seq'}, use_global_device_ids=true, to_apply=%region_5.6 | all-reduce | flops 128 | bytes 1024 | tf_op jit(solution)/shard_map/psum | solution.py:68
  138.9 0.8 multiply_convert_fusion
  139.7 38.9 %all-gather.5.cloned.1.call-done = bf16[5120,128]{0,1:T(8,128)(2,1)} async-done(((bf16[640,128]{0,1:T(8,128)(2,1)}), bf16[5120,128]{0,1:T(8,128)(2,1)}) %all-gather.5.cloned.1.call-update) | async-done | bytes 1310736 | tf_op jit(solution)/shard_map/all_gather | solution.py:72
  178.6 11.1 %convolution_bitcast_fusion.2 = f32[1728,128]{1,0:T(8,128)S(1)} fusion(bf16[5120,128]{0,1:T(8,128)(2,1)} %all-gather.5.cloned.1.call-done, bf16[1728,5120]{1,0:T(8,128)(2,1)} %param.17), kind=kOutput, calls=%fused_computation.3 | convolution fusion | flops 2264924160 | bytes 19890176 | tf_op jit(solution)/shard_map/dot_general | solution.py:73
  189.7 20.6 %convolution_bitcast_fusion = f32[5120,128]{0,1:T(8,128)} fusion(bf16[1728,5120]{1,0:T(8,128)(2,1)} %param.19, bf16[5120,128]{0,1:T(8,128)(2,1)S(1)} %copy-done.2, bf16[1728,5120]{1,0:T(8,128)(2,1)} %param.18, f32[1728,128]{1,0:T(8,128)S(1)} %convolution_bitcast_fusion.2), kind=kOutput, calls=%fused_computation | convolution fusion | flops 4531175424 | bytes 40206336 | tf_op jit(solution)/shard_map/dot_general | solution.py:76
  210.4 69.7 %reduce-scatter.2.cloned.1.call-done = f32[640,128]{0,1:T(8,128)} async-done(((f32[5120,128]{0,1:T(8,128)}), f32[640,128]{0,1:T(8,128)}) %reduce-scatter.2.cloned.1.call-update) | async-done | bytes 327696 | tf_op jit(solution)/shard_map/reduce_scatter | solution.py:79
  280.1 1.0 fusion.13
  281.1 0.8 copy.40
  (28 shorter events, 0.4 us)
Async XLA Ops:
  6.5 67.1 %copy-start = (bf16[64,640]{1,0:T(8,128)(2,1)S(1)}, bf16[64,640]{1,0:T(8,128)(2,1)}, u32[]{:S(2)}) copy-start(bf16[64,640]{1,0:T(8,128)(2,1)} %param.10) | copy-start | bytes 245764
  6.5 66.8 %copy-start.5 = (s32[16]{0:T(128)S(1)}, s32[16]{0:T(128)}, u32[]{:S(2)}) copy-start(s32[16]{0:T(128)} %param.13) | copy-start | bytes 196
  6.5 108.1 %all-gather.3.cloned.1.call-start = ((), (), s32[]{:S(2)}) async-start(), calls=%async_computation.2 | async-start | bytes 4096000 | tf_op jit(solution)/shard_map/all_gather | solution.py:61
  41.1 37.7 %copy-start.3 = (bf16[1,640,128]{2,1,0:T(8,128)(2,1)S(1)}, bf16[1,640,128]{2,1,0:T(8,128)(2,1)}, u32[]{:S(2)}) copy-start(bf16[1,640,128]{2,1,0:T(8,128)(2,1)} %param.15) | copy-start | bytes 491524
  73.1 5.9 %copy-start.4 = (bf16[640]{0:T(1024)(128)(2,1)S(1)}, bf16[640]{0:T(1024)(128)(2,1)}, u32[]{:S(2)}) copy-start(bf16[640]{0:T(1024)(128)(2,1)} %param.16) | copy-start | bytes 3844
  75.5 7.5 %all-to-all-start = ((bf16[4,16,640]{2,1,0:T(8,128)(2,1)}), bf16[4,16,640]{2,1,0:T(8,128)(2,1)S(1)}, u32[]{:S(2)}, u32[]{:S(2)}) async-start(bf16[4,16,640]{2,1,0:T(8,128)(2,1)} %reshape_reshape.3), calls=%async_computation | async-start | bytes 163840 | tf_op jit(solution)/shard_map/all_to_all | solution.py:60
  78.8 99.8 %all-gather.5.cloned.1.call-start = ((), (), s32[]{:S(2)}) async-start(), calls=%async_computation.3 | async-start | bytes 1474560 | tf_op jit(solution)/shard_map/all_gather | solution.py:72
  139.7 140.4 %reduce-scatter.2.cloned.1.call-start = ((), (), s32[]{:S(2)}) async-start(), calls=%async_computation.4 | async-start | bytes 2949120 | tf_op jit(solution)/shard_map/reduce_scatter | solution.py:79
  178.6 11.1 %copy-start.2 = (bf16[5120,128]{0,1:T(8,128)(2,1)S(1)}, bf16[5120,128]{0,1:T(8,128)(2,1)}, u32[]{:S(2)}) copy-start(bf16[5120,128]{0,1:T(8,128)(2,1)} %all-gather.5.cloned.1.call-done) | copy-start | bytes 3932164
  189.7 92.2 %copy-start.1 = (bf16[64,640]{1,0:T(8,128)(2,1)S(1)}, bf16[64,640]{1,0:T(8,128)(2,1)}, u32[]{:S(2)}) copy-start(bf16[64,640]{1,0:T(8,128)(2,1)} %param.10) | copy-start | bytes 245764
Sparse Core Ops, SparseCore 0:
  8.9 31.9 all-gather.2
  139.8 38.8 all-gather.4
  210.5 69.5 reduce-scatter.1
where the time goes:
time: 289 us; the launch traced here: 288 us
  blocking collectives  119 us (41%)
  waiting for transfers between devices  113 us (39%)
  matrix products  35.1 us (12%)
  between operations  13.3 us (5%)
  starting transfers between devices  3.38 us (1%)
    reduce_scatter x1, waiting for transfers between devices, on_device(): down = lax.psum_scatter(term, 'seq', scatter_dimension=0, tiled=True)  69.7 us
    all_gather x1, waiting for transfers between devices, on_device(): piece = lax.all_gather(normed, 'seq', axis=0, tiled=True)  38.9 us
    all_gather x1, blocking collectives, on_device(): key_piece = lax.all_gather(keys, 'seq', axis=0, tiled=True)  33.6 us
    all_gather x1, blocking collectives, on_device(): value_piece = lax.all_gather(values, 'seq', axis=0, tiled=True)  31.9 us
    all_gather x1, blocking collectives, on_device(): piece = lax.all_gather(group_rows, 'seq', axis=0, tiled=True)  31.7 us
    psum x1, blocking collectives, on_device(): squares = lax.psum(jnp.sum(carried * carried, axis=0), 'seq')  21.5 us
    dot_general x1, matrix products, on_device(): lax.dot_general(w_down, hidden, (((0,), (0,)), ((), ())), preferred_eleme...  20.6 us
    dot_general x1, matrix products, on_device(): gate_sum = jnp.dot(w_gate, piece, preferred_element_type=jnp.float32)  11.1 us
  transfers between devices with their start and end apart: 4, of which 3 were waited for; matrix products, arithmetic and copies ran while one was open for 1% of the time, Pallas kernels for 0%

commit v1 on v0

--- a/solution.py
+++ b/solution.py
@@ -27,7 +27,9 @@
     query_heads = queries.reshape(seq_dev, heads_dev, HEAD_DIM)
     scale = HEAD_DIM ** (-0.5)
     running_max = jnp.full((seq_dev, heads_dev), -1e30, jnp.float32)
-    key_piece = lax.all_gather(keys, "seq", axis=0, tiled=True)
+    key_piece = jnp.concatenate(
+        lax.all_to_all(jnp.stack([keys] * lax.axis_size("seq")), "seq", 0, 0), axis=0
+    )
     value_piece = lax.all_gather(values, "seq", axis=0, tiled=True)
     count = key_piece.shape[0]
     key_pos = key_positions(block_order, jnp.int32(0), count, block_rows)

time: 289 us -> 271 us (0.938)
  blocking collectives: 119 us -> 90.7 us
  starting transfers between devices: 3.38 us -> 10.7 us
    all_gather x1 -> x0, blocking collectives: 33.6 us -> none  [on_device(): key_piece = lax.all_gather(keys, 'seq', axis=0, tiled=True)]
    all_gather x1, blocking collectives: 31.9 us -> 41 us  [on_device(): value_piece = lax.all_gather(values, 'seq', axis=0, tiled=True)]
    all_to_all x0 -> x1, starting transfers between devices: none -> 7.31 us  [on_device(): lax.all_to_all(jnp.stack([keys] * lax.axis_size('seq')), 'seq', 0, 0)]
    psum x1, blocking collectives: 21.5 us -> 17.8 us  [on_device(): squares = lax.psum(jnp.sum(carried * carried, axis=0), 'seq')]
  transfers between devices with their start and end apart: 4 -> 5, of which waited for: 3 -> 3; matrix products, arithmetic and copies ran while one was open for 1% -> 2% of each run, Pallas kernels for 0% -> 0%
where the time goes in v1:
time: 271 us
  waiting for transfers between devices  114 us (42%)
  blocking collectives  90.7 us (33%)
  matrix products  35.2 us (13%)
  between operations  13.3 us (5%)
  starting transfers between devices  10.7 us (4%)
  local copies, waits for them, and re-layouts  4.58 us (2%)
    reduce_scatter x1, waiting for transfers between devices, on_device(): down = lax.psum_scatter(term, 'seq', scatter_dimension=0, tiled=True)  69.5 us
    all_gather x1, blocking collectives, on_device(): value_piece = lax.all_gather(values, 'seq', axis=0, tiled=True)  41 us
    all_gather x1, waiting for transfers between devices, on_device(): piece = lax.all_gather(normed, 'seq', axis=0, tiled=True)  39.7 us
    all_gather x1, blocking collectives, on_device(): piece = lax.all_gather(group_rows, 'seq', axis=0, tiled=True)  31.8 us
    dot_general x1, matrix products, on_device(): lax.dot_general(w_down, hidden, (((0,), (0,)), ((), ())), preferred_eleme...  20.6 us
    psum x1, blocking collectives, on_device(): squares = lax.psum(jnp.sum(carried * carried, axis=0), 'seq')  17.8 us
    dot_general x1, matrix products, on_device(): gate_sum = jnp.dot(w_gate, piece, preferred_element_type=jnp.float32)  11.1 us
    all_to_all x1, starting transfers between devices, on_device(): lax.all_to_all(jnp.stack([keys] * lax.axis_size('seq')), 'seq', 0, 0)  7.31 us
  transfers between devices with their start and end apart: 5, of which 3 were waited for; matrix products, arithmetic and copies ran while one was open for 2% of the time, Pallas kernels for 0%

profile of v1, /device:TPU:0, one launch (start us, length us, event | category | flops | bytes accessed | tf_op | source)
XLA Modules:
  0.0 270.8 jit_solution(10974706839600329962)
XLA Ops:
  6.5 0.7 all-gather.3.cloned.1.call-update
  7.3 1.8 stack.2
  9.0 7.3 %all-to-all-start = ((bf16[8,64,640]{2,1,0:T(8,128)(2,1)}), bf16[8,64,640]{2,1,0:T(8,128)(2,1)S(1)}, u32[]{:S(2)}, u32[]{:S(2)}) async-start(bf16[8,64,640]{2,1,0:T(8,128)(2,1)} %stack.2), calls=%async_computation | async-start | bytes 1310720 | tf_op jit(solution)/shard_map/all_to_all | solution.py:31
  16.3 41.0 %all_gather.12 = bf16[512,640]{1,0:T(8,128)(2,1)S(1)} all-gather(bf16[64,640]{1,0:T(8,128)(2,1)} %param.12), channel_id=1, replica_groups=mesh['section'=2,'seq'=8,'rep'=2] {'seq'}, dimensions={0}, use_global_device_ids=true | all-gather | bytes 737280 | tf_op jit(solution)/shard_map/all_gather | solution.py:33
  57.4 0.3 copy.33
  57.7 0.1 select_reduce_fusion.2
  58.0 0.7 reshape_reshape.6
  58.8 0.4 select_reduce_fusion
  59.2 0.3 fusion.7
  59.5 0.4 fusion.5
  60.0 0.7 reshape_reshape.7
  60.7 3.3 %all-to-all-start.1 = ((bf16[4,16,640]{2,1,0:T(8,128)(2,1)}), bf16[4,16,640]{2,1,0:T(8,128)(2,1)S(1)}, u32[]{:S(2)}, u32[]{:S(2)}) async-start(bf16[4,16,640]{2,1,0:T(8,128)(2,1)} %reshape_reshape.7), calls=%async_computation.1 | async-start | bytes 163840 | tf_op jit(solution)/shard_map/all_to_all | solution.py:62
  64.1 0.2 copy.30
  64.3 3.9 %all-to-all-done.1 = bf16[4,16,640]{2,1,0:T(8,128)(2,1)S(1)} async-done(((bf16[4,16,640]{2,1,0:T(8,128)(2,1)}), bf16[4,16,640]{2,1,0:T(8,128)(2,1)S(1)}, u32[]{:S(2)}, u32[]{:S(2)}) %all-to-all-start.1) | async-done | bytes 81952 | tf_op jit(solution)/shard_map/all_to_all | solution.py:62
  68.2 31.8 %all_gather.13 = bf16[8,16,2560]{2,1,0:T(8,128)(2,1)S(1)} all-gather(bf16[1,16,2560]{2,1,0:T(8,128)(2,1)S(1)} %bitcast.56), channel_id=1, replica_groups=mesh['section'=2,'seq'=8,'rep'=2] {'seq'}, dimensions={0}, use_global_device_ids=true | all-gather | bytes 737280 | tf_op jit(solution)/shard_map/all_gather | solution.py:64
  100.0 2.7 multiply_reduce_fusion
  102.7 17.8 %psum.7 = f32[128]{0:T(128)S(1)} all-reduce(f32[128]{0:T(128)S(1)} %get-tuple-element.7), channel_id=1, replica_groups=mesh['section'=2,'seq'=8,'rep'=2] {'seq'}, use_global_device_ids=true, to_apply=%region_5.6 | all-reduce | flops 128 | bytes 1024 | tf_op jit(solution)/shard_map/psum | solution.py:70
  120.6 0.8 multiply_convert_fusion
  121.4 39.7 %all-gather.5.cloned.1.call-done = bf16[5120,128]{0,1:T(8,128)(2,1)} async-done(((bf16[640,128]{0,1:T(8,128)(2,1)}), bf16[5120,128]{0,1:T(8,128)(2,1)}) %all-gather.5.cloned.1.call-update) | async-done | bytes 1310736 | tf_op jit(solution)/shard_map/all_gather | solution.py:74
  161.1 11.1 %convolution_bitcast_fusion.2 = f32[1728,128]{1,0:T(8,128)S(1)} fusion(bf16[5120,128]{0,1:T(8,128)(2,1)} %all-gather.5.cloned.1.call-done, bf16[1728,5120]{1,0:T(8,128)(2,1)} %param.17), kind=kOutput, calls=%fused_computation.3 | convolution fusion | flops 2264924160 | bytes 19890176 | tf_op jit(solution)/shard_map/dot_general | solution.py:75
  172.2 20.6 %convolution_bitcast_fusion = f32[5120,128]{0,1:T(8,128)} fusion(bf16[1728,5120]{1,0:T(8,128)(2,1)} %param.19, bf16[5120,128]{0,1:T(8,128)(2,1)S(1)} %copy-done.2, bf16[1728,5120]{1,0:T(8,128)(2,1)} %param.18, f32[1728,128]{1,0:T(8,128)S(1)} %convolution_bitcast_fusion.2), kind=kOutput, calls=%fused_computation | convolution fusion | flops 4531175424 | bytes 40206336 | tf_op jit(solution)/shard_map/dot_general | solution.py:78
  192.9 69.5 %reduce-scatter.2.cloned.1.call-done = f32[640,128]{0,1:T(8,128)} async-done(((f32[5120,128]{0,1:T(8,128)}), f32[640,128]{0,1:T(8,128)}) %reduce-scatter.2.cloned.1.call-update) | async-done | bytes 327696 | tf_op jit(solution)/shard_map/reduce_scatter | solution.py:81
  262.4 1.0 fusion.14
  263.4 0.8 copy.37
  (30 shorter events, 0.4 us)
Async XLA Ops:
  6.5 52.2 %copy-start = (bf16[64,640]{1,0:T(8,128)(2,1)S(1)}, bf16[64,640]{1,0:T(8,128)(2,1)}, u32[]{:S(2)}) copy-start(bf16[64,640]{1,0:T(8,128)(2,1)} %param.10) | copy-start | bytes 245764
  6.5 51.1 %copy-start.5 = (s32[16]{0:T(128)S(1)}, s32[16]{0:T(128)}, u32[]{:S(2)}) copy-start(s32[16]{0:T(128)} %param.13) | copy-start | bytes 196
  6.5 93.5 %all-gather.3.cloned.1.call-start = ((), (), s32[]{:S(2)}) async-start(), calls=%async_computation.3 | async-start | bytes 4096000 | tf_op jit(solution)/shard_map/all_gather | solution.py:63
  9.0 49.0 %all-to-all-start = ((bf16[8,64,640]{2,1,0:T(8,128)(2,1)}), bf16[8,64,640]{2,1,0:T(8,128)(2,1)S(1)}, u32[]{:S(2)}, u32[]{:S(2)}) async-start(bf16[8,64,640]{2,1,0:T(8,128)(2,1)} %stack.2), calls=%async_computation | async-start | bytes 1310720 | tf_op jit(solution)/shard_map/all_to_all | solution.py:31
  58.0 6.1 %copy-start.3 = (bf16[1,640,128]{2,1,0:T(8,128)(2,1)S(1)}, bf16[1,640,128]{2,1,0:T(8,128)(2,1)}, u32[]{:S(2)}) copy-start(bf16[1,640,128]{2,1,0:T(8,128)(2,1)} %param.15) | copy-start | bytes 491524
  58.0 6.2 %copy-start.4 = (bf16[640]{0:T(1024)(128)(2,1)S(1)}, bf16[640]{0:T(1024)(128)(2,1)}, u32[]{:S(2)}) copy-start(bf16[640]{0:T(1024)(128)(2,1)} %param.16) | copy-start | bytes 3844
  60.7 7.5 %all-to-all-start.1 = ((bf16[4,16,640]{2,1,0:T(8,128)(2,1)}), bf16[4,16,640]{2,1,0:T(8,128)(2,1)S(1)}, u32[]{:S(2)}, u32[]{:S(2)}) async-start(bf16[4,16,640]{2,1,0:T(8,128)(2,1)} %reshape_reshape.7), calls=%async_computation.1 | async-start | bytes 163840 | tf_op jit(solution)/shard_map/all_to_all | solution.py:62
  64.0 97.1 %all-gather.5.cloned.1.call-start = ((), (), s32[]{:S(2)}) async-start(), calls=%async_computation.4 | async-start | bytes 1474560 | tf_op jit(solution)/shard_map/all_gather | solution.py:74
  121.4 141.1 %reduce-scatter.2.cloned.1.call-start = ((), (), s32[]{:S(2)}) async-start(), calls=%async_computation.5 | async-start | bytes 2949120 | tf_op jit(solution)/shard_map/reduce_scatter | solution.py:81
  161.1 11.1 %copy-start.2 = (bf16[5120,128]{0,1:T(8,128)(2,1)S(1)}, bf16[5120,128]{0,1:T(8,128)(2,1)}, u32[]{:S(2)}) copy-start(bf16[5120,128]{0,1:T(8,128)(2,1)} %all-gather.5.cloned.1.call-done) | copy-start | bytes 3932164
  172.2 92.0 %copy-start.1 = (bf16[64,640]{1,0:T(8,128)(2,1)S(1)}, bf16[64,640]{1,0:T(8,128)(2,1)}, u32[]{:S(2)}) copy-start(bf16[64,640]{1,0:T(8,128)(2,1)} %param.10) | copy-start | bytes 245764
Sparse Core Ops, SparseCore 0:
  8.9 31.9 all-gather.2
  121.5 39.5 all-gather.4
  193.0 69.3 reduce-scatter.1
